TPU v7x, 32 devices: a whole 2x2x4 slice. The times are simulated.
32 devices in a mesh: lat: 8 (over z, y), ch: 4 (over x, core).
Axes of the slice: x: 2, y: 2, z: 4, core: 2. Of those that a mesh axis runs over, the one named last changes fastest.
Arguments:
- field: bfloat16 [728, 256, 1440], P('lat', 'ch'), may hold values from -6 to 6
- legendre: bfloat16 [384, 721, 728], P(('lat', 'ch')), may hold values from -0.21875 to 0.21875
- pair_order: int32 [384], replicated, may hold values from 0 to 383, each once
Outputs:
- coeffs: float32 [384, 721, 2, 256], P(('lat', 'ch'))
Inputs may be any that keep to these rules, and one draw needn't show every extreme that they name: `pair_order`: each of 0 to 383 appears once; a value p below 360 gives its bin the orders p and 719 - p, and a bin with a larger value is empty.
All inputs are finite; a program needn't handle non-finite values.
Results may differ from a plain program's by a relative error of at most 0.0037.
Values may be sent and summed in bfloat16 or wider, within the bound.
A program may use at most 256 MiB of HBM per device.

v0:
```python
import math
import jax
import jax.numpy as jnp
from jax import lax
from jax.sharding import PartitionSpec as P

NLAT = 721
GROUPS = 4


def dft_table(points, modes, lon_count):
    columns = jnp.repeat(modes, 2)
    phase = jnp.tile(jnp.array([0, lon_count // 4], jnp.int32), modes.shape[0])
    turns = (points[:, None] * columns[None, :] + phase[None, :]) % lon_count
    angle = turns.astype(jnp.float32) * (2.0 * math.pi / lon_count)
    return jnp.cos(angle).astype(jnp.bfloat16)


def per_device(field, legendre, pair_order):
    lat_rows, chan_dev, lon_count = field.shape
    own, row_count, _ = legendre.shape
    lat_count = lax.axis_size("lat")
    ch_count = lax.axis_size("ch")
    dev_count = lat_count * ch_count
    me = lax.axis_index("lat") * ch_count + lax.axis_index("ch")
    max_order = row_count - 1
    keep_all = pair_order < max_order // 2
    first_order = jnp.where(keep_all, pair_order, 0)
    orders = jnp.stack([first_order, max_order - 1 - first_order], axis=1)
    bound_own = lax.dynamic_slice_in_dim(max_order - first_order, me * own, own)
    keep_own = lax.dynamic_slice_in_dim(keep_all, me * own, own)
    rows_global = lax.axis_index("lat") * lat_rows + jnp.arange(lat_rows, dtype=jnp.int32)
    in_grid = (rows_global < NLAT)[:, None, None]
    norm_scale = 2.0 * math.pi / lon_count
    points = jnp.arange(lon_count, dtype=jnp.int32)
    degree = jnp.arange(row_count, dtype=jnp.int32)
    groups = math.gcd(GROUPS, own)
    width = own // groups
    by_dev = orders.reshape(dev_count, own, 2)
    outs = []
    for g in range(groups):
        part = by_dev[:, g * width : (g + 1) * width].reshape(-1)
        basis = dft_table(points, part, lon_count)
        fourier = jnp.einsum("ack,kn->anc", field, basis, preferred_element_type=jnp.float32)
        fourier = jnp.where(in_grid, fourier * norm_scale, 0.0).astype(jnp.bfloat16)
        fourier = fourier.reshape(lat_rows, dev_count * width, 4 * chan_dev)
        got = lax.all_to_all(fourier, ("lat", "ch"), split_axis=1, concat_axis=0, tiled=True)
        got = got.reshape(lat_count, ch_count, lat_rows, width, 4, chan_dev)
        got = got.transpose(3, 0, 2, 4, 1, 5)
        got = got.reshape(width, lat_count * lat_rows, 4 * ch_count * chan_dev)
        products = jnp.einsum(
            "brl,bln->brn",
            legendre[g * width : (g + 1) * width],
            got,
            preferred_element_type=jnp.float32,
        )
        bound = bound_own[g * width : (g + 1) * width]
        keep = keep_own[g * width : (g + 1) * width]
        upper = degree[None, :, None] < bound[:, None, None]
        half = products.shape[2] // 2
        chosen = jnp.where(upper, products[:, :, :half], products[:, :, half:])
        chosen = chosen * keep[:, None, None].astype(jnp.float32)
        outs.append(chosen.reshape(width, row_count, 2, half // 2))
    return outs[0] if groups == 1 else jnp.concatenate(outs, axis=0)


def solution(mesh):
    in_specs = (P("lat", "ch", None), P(("lat", "ch"), None, None), P())
    out_specs = P(("lat", "ch"), None, None, None)
    return jax.shard_map(
        per_device, mesh=mesh, in_specs=in_specs, out_specs=out_specs, check_vma=False
    )
```

profile of v0, /device:TPU:0, one launch (start us, length us, event | category | flops | bytes accessed | tf_op | source)
XLA Modules:
  0.0 631.1 jit_solution(3836355545497258501)
XLA Ops:
  0.0 0.7 broadcast_subtract_fusion.1
  1.2 0.1 reshape.192
  1.5 0.1 mul.134
  1.8 41.2 %fusion.8 = bf16[91,384,64]{1,0,2:T(8,128)(2,1)} fusion(pred[91]{0:T(512)(128)(4,1)S(1)} %add_compare_fusion, bf16[91,64,1440]{2,1,0:T(8,128)(2,1)} %param.7, s32[384]{0:T(512)S(1)} %add.79, s32[384]{0:T(512)S(1)} %mul.134), kind=kOutput, calls=%fused_computation.13 | convolution fusion | flops 6453669888 | bytes 21249116 | tf_op jit(solution)/shard_map/ack,kn->anc/dot_general | solution.py:44
  42.9 8.6 %copy.44 = bf16[91,384,64]{0,2,1:T(8,128)(2,1)} copy(bf16[91,384,64]{1,0,2:T(8,128)(2,1)} %fusion.8) | data formatting | bytes 8945664 | tf_op jit(solution)/shard_map/convert_element_type | solution.py:45
  51.5 8.3 %copy.45 = bf16[91,96,256]{2,0,1:T(8,128)(2,1)} copy(bf16[91,96,256]{0,2,1:T(8,128)(2,1)} %bitcast.80) | data formatting | bytes 8945664 | tf_op jit(solution)/shard_map/reshape | solution.py:46
  59.8 7.7 %all-to-all-start = ((bf16[91,96,256]{2,0,1:T(8,128)(2,1)}), bf16[91,96,256]{2,0,1:T(8,128)(2,1)}, u32[]{:S(2)}, u32[]{:S(2)}) async-start(bf16[91,96,256]{2,0,1:T(8,128)(2,1)} %copy.45), calls=%async_computation | async-start | bytes 9437184 | tf_op jit(solution)/shard_map/all_to_all | solution.py:47
  67.7 0.1 reshape.197
  68.1 41.2 %fusion.9 = bf16[91,384,64]{1,0,2:T(8,128)(2,1)} fusion(pred[91]{0:T(512)(128)(4,1)S(1)} %add_compare_fusion, bf16[91,64,1440]{2,1,0:T(8,128)(2,1)} %param.7, s32[384]{0:T(512)S(1)} %mul.142, s32[384]{0:T(512)S(1)} %add.79), kind=kOutput, calls=%fused_computation.14 | convolution fusion | flops 6453669888 | bytes 21249116 | tf_op jit(solution)/shard_map/ack,kn->anc/dot_general | solution.py:44
  109.3 8.6 %copy.51 = bf16[91,384,64]{0,2,1:T(8,128)(2,1)} copy(bf16[91,384,64]{1,0,2:T(8,128)(2,1)} %fusion.9) | data formatting | bytes 8945664 | tf_op jit(solution)/shard_map/convert_element_type | solution.py:45
  117.9 8.3 %copy.52 = bf16[91,96,256]{2,0,1:T(8,128)(2,1)} copy(bf16[91,96,256]{0,2,1:T(8,128)(2,1)} %bitcast.81) | data formatting | bytes 8945664 | tf_op jit(solution)/shard_map/reshape | solution.py:46
  126.2 46.4 %all-to-all-done = bf16[91,96,256]{2,0,1:T(8,128)(2,1)} async-done(((bf16[91,96,256]{2,0,1:T(8,128)(2,1)}), bf16[91,96,256]{2,0,1:T(8,128)(2,1)}, u32[]{:S(2)}, u32[]{:S(2)}) %all-to-all-start) | async-done | bytes 4472864 | tf_op jit(solution)/shard_map/all_to_all | solution.py:47
  172.6 4.6 all-to-all-start.1
  177.3 0.1 reshape.202
  177.7 41.3 %fusion.10 = bf16[91,384,64]{1,0,2:T(8,128)(2,1)} fusion(pred[91]{0:T(512)(128)(4,1)S(1)} %add_compare_fusion, bf16[91,64,1440]{2,1,0:T(8,128)(2,1)} %param.7, s32[384]{0:T(512)S(1)} %mul.150, s32[384]{0:T(512)S(1)} %add.79), kind=kOutput, calls=%fused_computation.15 | convolution fusion | flops 6453669888 | bytes 21249116 | tf_op jit(solution)/shard_map/ack,kn->anc/dot_general | solution.py:44
  219.0 8.6 %copy.58 = bf16[91,384,64]{0,2,1:T(8,128)(2,1)} copy(bf16[91,384,64]{1,0,2:T(8,128)(2,1)} %fusion.10) | data formatting | bytes 8945664 | tf_op jit(solution)/shard_map/convert_element_type | solution.py:45
  227.6 8.3 %copy.59 = bf16[91,96,256]{2,0,1:T(8,128)(2,1)} copy(bf16[91,96,256]{0,2,1:T(8,128)(2,1)} %bitcast.82) | data formatting | bytes 8945664 | tf_op jit(solution)/shard_map/reshape | solution.py:46
  235.9 46.4 %all-to-all-done.1 = bf16[91,96,256]{2,0,1:T(8,128)(2,1)} async-done(((bf16[91,96,256]{2,0,1:T(8,128)(2,1)}), bf16[91,96,256]{2,0,1:T(8,128)(2,1)}, u32[]{:S(2)}, u32[]{:S(2)}) %all-to-all-start.1) | async-done | bytes 4472864 | tf_op jit(solution)/shard_map/all_to_all | solution.py:47
  282.3 4.3 all-to-all-start.2
  286.7 0.1 reshape.207
  287.1 41.2 %fusion.11 = bf16[91,384,64]{1,0,2:T(8,128)(2,1)} fusion(pred[91]{0:T(512)(128)(4,1)S(1)} %add_compare_fusion, bf16[91,64,1440]{2,1,0:T(8,128)(2,1)} %param.7, s32[384]{0:T(512)S(1)} %mul.158, s32[384]{0:T(512)S(1)} %add.79), kind=kOutput, calls=%fused_computation.16 | convolution fusion | flops 6453669888 | bytes 21249116 | tf_op jit(solution)/shard_map/ack,kn->anc/dot_general | solution.py:44
  328.3 8.6 %copy.65 = bf16[91,384,64]{0,2,1:T(8,128)(2,1)} copy(bf16[91,384,64]{1,0,2:T(8,128)(2,1)} %fusion.11) | data formatting | bytes 8945664 | tf_op jit(solution)/shard_map/convert_element_type | solution.py:45
  336.9 8.3 %copy.66 = bf16[91,96,256]{2,0,1:T(8,128)(2,1)} copy(bf16[91,96,256]{0,2,1:T(8,128)(2,1)} %bitcast.83) | data formatting | bytes 8945664 | tf_op jit(solution)/shard_map/reshape | solution.py:46
  345.2 46.4 %all-to-all-done.2 = bf16[91,96,256]{2,0,1:T(8,128)(2,1)} async-done(((bf16[91,96,256]{2,0,1:T(8,128)(2,1)}), bf16[91,96,256]{2,0,1:T(8,128)(2,1)}, u32[]{:S(2)}, u32[]{:S(2)}) %all-to-all-start.2) | async-done | bytes 4472864 | tf_op jit(solution)/shard_map/all_to_all | solution.py:47
  391.6 4.1 all-to-all-start.3
  396.3 8.2 %copy.46 = bf16[32,91,3,256]{1,3,2,0:T(8,128)(2,1)} copy(bf16[32,91,3,256]{3,1,2,0:T(8,128)(2,1)} %bitcast.4) | data formatting | bytes 8945664 | tf_op jit(solution)/shard_map/all_to_all | solution.py:47
  404.6 18.3 %copy.47 = bf16[3,8,91,4,4,64]{2,1,5,4,3,0:T(8,128)(2,1)} copy(bf16[3,8,91,4,4,64]{2,5,3,0,4,1:T(8,128)(2,1)} %bitcast.76) | data formatting | bytes 8945664 | tf_op jit(solution)/shard_map/transpose | solution.py:49
  422.9 10.7 %reshape.217 = bf16[3,728,1024]{1,2,0:T(8,128)(2,1)} reshape(bf16[3,8,91,4,4,64]{2,1,5,4,3,0:T(8,128)(2,1)} %copy.47) | data formatting | bytes 8945664 | tf_op jit(solution)/shard_map/reshape | solution.py:50
  433.6 8.1 %copy.53 = bf16[32,91,3,256]{1,3,2,0:T(8,128)(2,1)} copy(bf16[32,91,3,256]{3,1,2,0:T(8,128)(2,1)} %bitcast.12) | data formatting | bytes 8945664 | tf_op jit(solution)/shard_map/all_to_all | solution.py:47
  441.6 18.1 %copy.54 = bf16[3,8,91,4,4,64]{2,1,5,4,3,0:T(8,128)(2,1)} copy(bf16[3,8,91,4,4,64]{2,5,3,0,4,1:T(8,128)(2,1)} %bitcast.77) | data formatting | bytes 8945664 | tf_op jit(solution)/shard_map/transpose | solution.py:49
  459.7 10.7 %reshape.219 = bf16[3,728,1024]{1,2,0:T(8,128)(2,1)} reshape(bf16[3,8,91,4,4,64]{2,1,5,4,3,0:T(8,128)(2,1)} %copy.54) | data formatting | bytes 8945664 | tf_op jit(solution)/shard_map/reshape | solution.py:50
  470.4 6.6 %fusion.24 = f32[3,721,1024]{2,1,0:T(8,128)S(1)} fusion(bf16[3,728,1024]{1,2,0:T(8,128)(2,1)} %reshape.217, bf16[12,721,728]{2,1,0:T(8,128)(2,1)} %param.8), kind=kOutput, calls=%fused_computation.33 | convolution fusion | flops 3224911872 | bytes 16932864 | tf_op jit(solution)/shard_map/brl,bln->brn/dot_general | solution.py:51
  477.0 6.6 %fusion.27 = f32[3,721,1024]{2,1,0:T(8,128)S(1)} fusion(bf16[3,728,1024]{1,2,0:T(8,128)(2,1)} %reshape.219, bf16[12,721,728]{2,1,0:T(8,128)(2,1)} %param.8), kind=kOutput, calls=%fused_computation.34 | convolution fusion | flops 3224911872 | bytes 16932864 | tf_op jit(solution)/shard_map/brl,bln->brn/dot_general | solution.py:51
  483.6 3.9 fusion.14
  487.5 6.4 %reshape.196 = f32[3,721,2,256]{3,2,1,0:T(2,128)} reshape(f32[3,721,512]{2,1,0:T(8,128)} %get-tuple-element.23) | data formatting | bytes 8859648 | tf_op jit(solution)/shard_map/reshape | solution.py:63
  493.9 6.4 %reshape.201 = f32[3,721,2,256]{3,2,1,0:T(2,128)} reshape(f32[3,721,512]{2,1,0:T(8,128)} %get-tuple-element.22) | data formatting | bytes 8859648 | tf_op jit(solution)/shard_map/reshape | solution.py:63
  500.2 8.2 %copy.60 = bf16[32,91,3,256]{1,3,2,0:T(8,128)(2,1)} copy(bf16[32,91,3,256]{3,1,2,0:T(8,128)(2,1)} %bitcast.20) | data formatting | bytes 8945664 | tf_op jit(solution)/shard_map/all_to_all | solution.py:47
  508.5 18.4 %copy.61 = bf16[3,8,91,4,4,64]{2,1,5,4,3,0:T(8,128)(2,1)} copy(bf16[3,8,91,4,4,64]{2,5,3,0,4,1:T(8,128)(2,1)} %bitcast.78) | data formatting | bytes 8945664 | tf_op jit(solution)/shard_map/transpose | solution.py:49
  526.9 10.7 %reshape.221 = bf16[3,728,1024]{1,2,0:T(8,128)(2,1)} reshape(bf16[3,8,91,4,4,64]{2,1,5,4,3,0:T(8,128)(2,1)} %copy.61) | data formatting | bytes 8945664 | tf_op jit(solution)/shard_map/reshape | solution.py:50
  537.5 10.5 %fusion.30 = f32[3,721,1024]{2,1,0:T(8,128)} fusion(bf16[3,728,1024]{1,2,0:T(8,128)(2,1)} %reshape.221, bf16[12,721,728]{2,1,0:T(8,128)(2,1)} %param.8), kind=kOutput, calls=%fused_computation.35 | convolution fusion | flops 3224911872 | bytes 16932864 | tf_op jit(solution)/shard_map/brl,bln->brn/dot_general | solution.py:51
  548.1 8.1 %copy.67 = bf16[32,91,3,256]{1,3,2,0:T(8,128)(2,1)} copy(bf16[32,91,3,256]{3,1,2,0:T(8,128)(2,1)} %bitcast.28) | data formatting | bytes 8945664 | tf_op jit(solution)/shard_map/all_to_all | solution.py:47
  556.1 18.1 %copy.68 = bf16[3,8,91,4,4,64]{2,1,5,4,3,0:T(8,128)(2,1)} copy(bf16[3,8,91,4,4,64]{2,5,3,0,4,1:T(8,128)(2,1)} %bitcast.79) | data formatting | bytes 8945664 | tf_op jit(solution)/shard_map/transpose | solution.py:49
  574.3 10.8 %reshape.223 = bf16[3,728,1024]{1,2,0:T(8,128)(2,1)} reshape(bf16[3,8,91,4,4,64]{2,1,5,4,3,0:T(8,128)(2,1)} %copy.68) | data formatting | bytes 8945664 | tf_op jit(solution)/shard_map/reshape | solution.py:50
  585.0 10.8 %fusion.33 = f32[3,721,1024]{2,1,0:T(8,128)} fusion(bf16[3,728,1024]{1,2,0:T(8,128)(2,1)} %reshape.223, bf16[12,721,728]{2,1,0:T(8,128)(2,1)} %param.8), kind=kOutput, calls=%fused_computation.36 | convolution fusion | flops 3224911872 | bytes 16932864 | tf_op jit(solution)/shard_map/brl,bln->brn/dot_general | solution.py:51
  595.8 8.4 %fusion.12 = (f32[3,721,512]{2,1,0:T(8,128)}, f32[3,721,512]{2,1,0:T(8,128)}) fusion(f32[3,721,1024]{2,1,0:T(8,128)} %fusion.33, f32[3]{0:T(128)S(1)} %get-tuple-element.17, pred[3,721]{1,0:T(4,128)(4,1)S(1)} %iota_compare_fusion, f32[3]{0:T(128)S(1)} %get-tuple-element.18, f32[3,721,1024]{2,1,0:T(8,128)S(1)} %bitcast.85, ...), kind=kLoop, calls=%fused_computation.18 | loop fusion | flops 4429824 | bytes 26583294 | tf_op jit(solution)/shard_map/mul | solution.py:62
  604.2 6.4 %reshape.206 = f32[3,721,2,256]{3,2,1,0:T(2,128)} reshape(f32[3,721,512]{2,1,0:T(8,128)} %get-tuple-element.21) | data formatting | bytes 8859648 | tf_op jit(solution)/shard_map/reshape | solution.py:63
  610.6 6.4 %reshape.211 = f32[3,721,2,256]{3,2,1,0:T(2,128)} reshape(f32[3,721,512]{2,1,0:T(8,128)} %get-tuple-element.20) | data formatting | bytes 8859648 | tf_op jit(solution)/shard_map/reshape | solution.py:63
  617.0 13.8 %pad_maximum_fusion = f32[12,721,2,256]{3,2,1,0:T(2,128)} fusion(f32[3,721,2,256]{3,2,1,0:T(2,128)} %reshape.211, f32[3,721,2,256]{3,2,1,0:T(2,128)} %reshape.206, f32[3,721,2,256]{3,2,1,0:T(2,128)} %reshape.201, f32[3,721,2,256]{3,2,1,0:T(2,128)} %reshape.196), kind=kLoop, calls=%fused_computation | loop fusion | flops 13289472 | bytes 35438592 | tf_op jit(solution)/shard_map/concatenate | solution.py:64
  (39 shorter events, 2.4 us)
Async XLA Ops:
  59.8 112.8 %all-to-all-start = ((bf16[91,96,256]{2,0,1:T(8,128)(2,1)}), bf16[91,96,256]{2,0,1:T(8,128)(2,1)}, u32[]{:S(2)}, u32[]{:S(2)}) async-start(bf16[91,96,256]{2,0,1:T(8,128)(2,1)} %copy.45), calls=%async_computation | async-start | bytes 9437184 | tf_op jit(solution)/shard_map/all_to_all | solution.py:47
  172.6 109.7 %all-to-all-start.1 = ((bf16[91,96,256]{2,0,1:T(8,128)(2,1)}), bf16[91,96,256]{2,0,1:T(8,128)(2,1)}, u32[]{:S(2)}, u32[]{:S(2)}) async-start(bf16[91,96,256]{2,0,1:T(8,128)(2,1)} %copy.52), calls=%async_computation.1 | async-start | bytes 9437184 | tf_op jit(solution)/shard_map/all_to_all | solution.py:47
  282.3 109.3 %all-to-all-start.2 = ((bf16[91,96,256]{2,0,1:T(8,128)(2,1)}), bf16[91,96,256]{2,0,1:T(8,128)(2,1)}, u32[]{:S(2)}, u32[]{:S(2)}) async-start(bf16[91,96,256]{2,0,1:T(8,128)(2,1)} %copy.59), calls=%async_computation.2 | async-start | bytes 9437184 | tf_op jit(solution)/shard_map/all_to_all | solution.py:47
  345.2 50.6 %copy-start = (s32[384]{0:T(512)S(1)}, s32[384]{0:T(512)}, u32[]{:S(2)}) copy-start(s32[384]{0:T(512)} %param.9) | copy-start | bytes 4612
  391.6 156.5 %all-to-all-start.3 = ((bf16[91,96,256]{2,0,1:T(8,128)(2,1)}), bf16[91,96,256]{2,0,1:T(8,128)(2,1)}, u32[]{:S(2)}, u32[]{:S(2)}) async-start(bf16[91,96,256]{2,0,1:T(8,128)(2,1)} %copy.66), calls=%async_computation.3 | async-start | bytes 9437184 | tf_op jit(solution)/shard_map/all_to_all | solution.py:47
  574.3 21.6 %slice-start = ((s8[8945664]{0:T(1024)(128)(4,1)}), s8[557056]{0:T(1024)(128)(4,1)S(1)}, s32[]{:S(2)}) async-start(s8[8945664]{0:T(1024)(128)(4,1)} %bitcast.84), calls=%async_computation.4 | async-start | bytes 1114112
  585.0 10.8 %slice-start.1 = ((s8[8945664]{0:T(1024)(128)(4,1)}), s8[4194304]{0:T(1024)(128)(4,1)S(1)}, s32[]{:S(2)}) async-start(s8[8945664]{0:T(1024)(128)(4,1)} %bitcast.84), calls=%async_computation.5 | async-start | bytes 8388608
  585.0 10.8 %slice-start.2 = ((s8[8945664]{0:T(1024)(128)(4,1)}), s8[4194304]{0:T(1024)(128)(4,1)S(1)}, s32[]{:S(2)}) async-start(s8[8945664]{0:T(1024)(128)(4,1)} %bitcast.84), calls=%async_computation.6 | async-start | bytes 8388608
where the time goes:
time: 641 us; the launch traced here: 631 us
  local copies, waits for them, and re-layouts  244 us (38%)
  matrix products  199 us (31%)
  waiting for transfers between devices  139 us (22%)
  other arithmetic  27.2 us (4%)
  starting transfers between devices  20.7 us (3%)
    dot_general x4, matrix products, per_device(): jnp.einsum('ack,kn->anc', field, basis, preferred_element_type=jnp.float32)  165 us
    all_to_all x4, waiting for transfers between devices, per_device(): lax.all_to_all(fourier, ('lat', 'ch'), split_axis=1, concat_axis=0, tiled...  139 us
    transpose x4, local copies, waits for them, and re-layouts, per_device(): got = got.transpose(3, 0, 2, 4, 1, 5)  72.9 us
    reshape x4, local copies, waits for them, and re-layouts, per_device(): got = got.reshape(width, lat_count * lat_rows, 4 * ch_count * chan_dev)  42.8 us
    dot_general x4, matrix products, per_device(): jnp.einsum('brl,bln->brn', legendre[g * width:(g + 1) * width], got, pref...  34.5 us
    convert_element_type x4, local copies, waits for them, and re-layouts, per_device(): fourier = jnp.where(in_grid, fourier * norm_scale, 0.0).astype(jnp.bfloat16)  34.4 us
    reshape x4, local copies, waits for them, and re-layouts, per_device(): fourier = fourier.reshape(lat_rows, dev_count * width, 4 * chan_dev)  33.2 us
    all_to_all x4, local copies, waits for them, and re-layouts, per_device(): lax.all_to_all(fourier, ('lat', 'ch'), split_axis=1, concat_axis=0, tiled...  32.6 us
  transfers between devices with their start and end apart: 4, of which 3 were waited for; matrix products, arithmetic and copies ran while one was open for 52% of the time, Pallas kernels for 0%

commit v1 on v0

--- a/solution.py
+++ b/solution.py
@@ -3,6 +3,7 @@
 import jax.numpy as jnp
 from jax import lax
 from jax.sharding import PartitionSpec as P
+from jax.lax import all_to_all, axis_size
 
 NLAT = 721
 GROUPS = 4
@@ -44,7 +45,14 @@
         fourier = jnp.einsum("ack,kn->anc", field, basis, preferred_element_type=jnp.float32)
         fourier = jnp.where(in_grid, fourier * norm_scale, 0.0).astype(jnp.bfloat16)
         fourier = fourier.reshape(lat_rows, dev_count * width, 4 * chan_dev)
-        got = lax.all_to_all(fourier, ("lat", "ch"), split_axis=1, concat_axis=0, tiled=True)
+
+        def streams_reach(original):
+            carry_in = jnp.split(original, axis_size(("lat", "ch")), axis=1)
+            response = jnp.stack(carry_in, axis=0)
+            placed = all_to_all(response, ("lat", "ch"), 0, 0)
+            return jnp.concatenate(placed, axis=0)
+
+        got = streams_reach(fourier)
         got = got.reshape(lat_count, ch_count, lat_rows, width, 4, chan_dev)
         got = got.transpose(3, 0, 2, 4, 1, 5)
         got = got.reshape(width, lat_count * lat_rows, 4 * ch_count * chan_dev)

time: 641 us -> 680 us (1.061)
  local copies, waits for them, and re-layouts: 244 us -> 394 us
  waiting for transfers between devices: 139 us -> 27.2 us
    unnamed x8 -> x140, local copies, waits for them, and re-layouts: 0.01 us -> 147 us
    all_to_all x4, waiting for transfers between devices: 139 us -> 27.2 us  [streams_reach(): placed = all_to_all(response, ('lat', 'ch'), 0, 0)]
    another operation x0 -> x8, local copies, waits for them, and re-layouts: none -> 36 us  [streams_reach(): response = jnp.stack(carry_in, axis=0)]
    reshape x4 -> x0, local copies, waits for them, and re-layouts: 33.2 us -> none  [per_device(): fourier = fourier.reshape(lat_rows, dev_count * width, 4 * chan_dev)]
  transfers between devices with their start and end apart: 4 -> 4, of which waited for: 3 -> 3; matrix products, arithmetic and copies ran while one was open for 52% -> 66% of each run, Pallas kernels for 0% -> 0%
where the time goes in v1:
time: 680 us; the launch traced here: 668 us
  local copies, waits for them, and re-layouts  394 us (58%)
  matrix products  199 us (29%)
  other arithmetic  27.2 us (4%)
  waiting for transfers between devices  27.2 us (4%)
  starting transfers between devices  20.5 us (3%)
    dot_general x4, matrix products, per_device(): jnp.einsum('ack,kn->anc', field, basis, preferred_element_type=jnp.float32)  165 us
    unnamed x140, local copies, waits for them, and re-layouts  147 us
    transpose x4, local copies, waits for them, and re-layouts, per_device(): got = got.transpose(3, 0, 2, 4, 1, 5)  72.4 us
    reshape x4, local copies, waits for them, and re-layouts, per_device(): got = got.reshape(width, lat_count * lat_rows, 4 * ch_count * chan_dev)  42.8 us
    another operation x8, local copies, waits for them, and re-layouts, streams_reach(): response = jnp.stack(carry_in, axis=0)  36 us
    dot_general x4, matrix products, per_device(): jnp.einsum('brl,bln->brn', legendre[g * width:(g + 1) * width], got, pref...  34.5 us
    convert_element_type x4, local copies, waits for them, and re-layouts, per_device(): fourier = jnp.where(in_grid, fourier * norm_scale, 0.0).astype(jnp.bfloat16)  34.4 us
    all_to_all x4, local copies, waits for them, and re-layouts, streams_reach(): placed = all_to_all(response, ('lat', 'ch'), 0, 0)  33 us
  transfers between devices with their start and end apart: 4, of which 3 were waited for; matrix products, arithmetic and copies ran while one was open for 66% of the time, Pallas kernels for 0%

profile of v1, /device:TPU:0, one launch (start us, length us, event | category | flops | bytes accessed | tf_op | source)
XLA Modules:
  0.0 668.3 jit_solution(9074618563427853704)
XLA Ops:
  1.8 41.2 %fusion.8 = bf16[91,384,64]{1,0,2:T(8,128)(2,1)} fusion(pred[91]{0:T(512)(128)(4,1)S(1)} %add_compare_fusion, bf16[91,64,1440]{2,1,0:T(8,128)(2,1)} %param.7, s32[384]{0:T(512)S(1)} %add.79, s32[384]{0:T(512)S(1)} %mul.134), kind=kOutput, calls=%fused_computation.13 | convolution fusion | flops 6453669888 | bytes 21249116 | tf_op jit(solution)/shard_map/ack,kn->anc/dot_general | solution.py:45
  43.0 8.6 %copy.36 = bf16[91,384,64]{0,2,1:T(8,128)(2,1)} copy(bf16[91,384,64]{1,0,2:T(8,128)(2,1)} %fusion.8) | data formatting | bytes 8945664 | tf_op jit(solution)/shard_map/convert_element_type | solution.py:46
  53.3 1.8 constant_dynamic-update-slice_fusion.30
  89.0 8.3 %copy.37 = bf16[32,91,3,256]{3,1,2,0:T(8,128)(2,1)} copy(bf16[32,91,3,256]{1,3,2,0:T(8,128)(2,1)} %constant_dynamic-update-slice_fusion) | data formatting | bytes 8945664 | tf_op jit(solution)/shard_map/stack | solution.py:51
  97.3 7.9 %all-to-all-start = ((bf16[32,91,3,256]{3,1,2,0:T(8,128)(2,1)}), bf16[32,91,3,256]{3,1,2,0:T(8,128)(2,1)}, u32[]{:S(2)}, u32[]{:S(2)}) async-start(bf16[32,91,3,256]{3,1,2,0:T(8,128)(2,1)} %copy.37), calls=%async_computation | async-start | bytes 9437184 | tf_op jit(solution)/shard_map/all_to_all | solution.py:52
  105.7 41.2 %fusion.9 = bf16[91,384,64]{1,0,2:T(8,128)(2,1)} fusion(pred[91]{0:T(512)(128)(4,1)S(1)} %add_compare_fusion, bf16[91,64,1440]{2,1,0:T(8,128)(2,1)} %param.7, s32[384]{0:T(512)S(1)} %mul.142, s32[384]{0:T(512)S(1)} %add.79), kind=kOutput, calls=%fused_computation.14 | convolution fusion | flops 6453669888 | bytes 21249116 | tf_op jit(solution)/shard_map/ack,kn->anc/dot_general | solution.py:45
  146.9 8.6 %copy.43 = bf16[91,384,64]{0,2,1:T(8,128)(2,1)} copy(bf16[91,384,64]{1,0,2:T(8,128)(2,1)} %fusion.9) | data formatting | bytes 8945664 | tf_op jit(solution)/shard_map/convert_element_type | solution.py:46
  155.5 1.8 constant_dynamic-update-slice_fusion.63
  157.2 1.8 constant_dynamic-update-slice_fusion.62
  192.9 8.3 %copy.44 = bf16[32,91,3,256]{3,1,2,0:T(8,128)(2,1)} copy(bf16[32,91,3,256]{1,3,2,0:T(8,128)(2,1)} %constant_dynamic-update-slice_fusion.32) | data formatting | bytes 8945664 | tf_op jit(solution)/shard_map/stack | solution.py:51
  201.7 8.6 %all-to-all-done = bf16[32,91,3,256]{3,1,2,0:T(8,128)(2,1)} async-done(((bf16[32,91,3,256]{3,1,2,0:T(8,128)(2,1)}), bf16[32,91,3,256]{3,1,2,0:T(8,128)(2,1)}, u32[]{:S(2)}, u32[]{:S(2)}) %all-to-all-start) | async-done | bytes 4472864 | tf_op jit(solution)/shard_map/all_to_all | solution.py:52
  210.2 4.3 all-to-all-start.1
  214.5 41.2 %fusion.10 = bf16[91,384,64]{1,0,2:T(8,128)(2,1)} fusion(pred[91]{0:T(512)(128)(4,1)S(1)} %add_compare_fusion, bf16[91,64,1440]{2,1,0:T(8,128)(2,1)} %param.7, s32[384]{0:T(512)S(1)} %mul.150, s32[384]{0:T(512)S(1)} %add.79), kind=kOutput, calls=%fused_computation.15 | convolution fusion | flops 6453669888 | bytes 21249116 | tf_op jit(solution)/shard_map/ack,kn->anc/dot_general | solution.py:45
  255.7 8.6 %copy.50 = bf16[91,384,64]{0,2,1:T(8,128)(2,1)} copy(bf16[91,384,64]{1,0,2:T(8,128)(2,1)} %fusion.10) | data formatting | bytes 8945664 | tf_op jit(solution)/shard_map/convert_element_type | solution.py:46
  264.3 1.8 constant_dynamic-update-slice_fusion.95
  266.0 1.8 constant_dynamic-update-slice_fusion.94
  301.7 8.3 %copy.51 = bf16[32,91,3,256]{3,1,2,0:T(8,128)(2,1)} copy(bf16[32,91,3,256]{1,3,2,0:T(8,128)(2,1)} %constant_dynamic-update-slice_fusion.64) | data formatting | bytes 8945664 | tf_op jit(solution)/shard_map/stack | solution.py:51
  310.5 9.0 %all-to-all-done.1 = bf16[32,91,3,256]{3,1,2,0:T(8,128)(2,1)} async-done(((bf16[32,91,3,256]{3,1,2,0:T(8,128)(2,1)}), bf16[32,91,3,256]{3,1,2,0:T(8,128)(2,1)}, u32[]{:S(2)}, u32[]{:S(2)}) %all-to-all-start.1) | async-done | bytes 4472864 | tf_op jit(solution)/shard_map/all_to_all | solution.py:52
  319.6 4.3 all-to-all-start.2
  323.9 41.2 %fusion.11 = bf16[91,384,64]{1,0,2:T(8,128)(2,1)} fusion(pred[91]{0:T(512)(128)(4,1)S(1)} %add_compare_fusion, bf16[91,64,1440]{2,1,0:T(8,128)(2,1)} %param.7, s32[384]{0:T(512)S(1)} %mul.158, s32[384]{0:T(512)S(1)} %add.79), kind=kOutput, calls=%fused_computation.16 | convolution fusion | flops 6453669888 | bytes 21249116 | tf_op jit(solution)/shard_map/ack,kn->anc/dot_general | solution.py:45
  365.0 8.6 %copy.57 = bf16[91,384,64]{0,2,1:T(8,128)(2,1)} copy(bf16[91,384,64]{1,0,2:T(8,128)(2,1)} %fusion.11) | data formatting | bytes 8945664 | tf_op jit(solution)/shard_map/convert_element_type | solution.py:46
  375.4 1.8 constant_dynamic-update-slice_fusion.126
  411.1 8.3 %copy.58 = bf16[32,91,3,256]{3,1,2,0:T(8,128)(2,1)} copy(bf16[32,91,3,256]{1,3,2,0:T(8,128)(2,1)} %constant_dynamic-update-slice_fusion.96) | data formatting | bytes 8945664 | tf_op jit(solution)/shard_map/stack | solution.py:51
  419.3 9.6 %all-to-all-done.2 = bf16[32,91,3,256]{3,1,2,0:T(8,128)(2,1)} async-done(((bf16[32,91,3,256]{3,1,2,0:T(8,128)(2,1)}), bf16[32,91,3,256]{3,1,2,0:T(8,128)(2,1)}, u32[]{:S(2)}, u32[]{:S(2)}) %all-to-all-start.2) | async-done | bytes 4472864 | tf_op jit(solution)/shard_map/all_to_all | solution.py:52
  428.9 4.1 all-to-all-start.3
  433.6 8.4 %copy.38 = bf16[32,91,3,256]{1,3,2,0:T(8,128)(2,1)} copy(bf16[32,91,3,256]{3,1,2,0:T(8,128)(2,1)} %all-to-all-done) | data formatting | bytes 8945664 | tf_op jit(solution)/shard_map/all_to_all | solution.py:52
  442.1 18.1 %copy.39 = bf16[3,8,91,4,4,64]{2,1,5,4,3,0:T(8,128)(2,1)} copy(bf16[3,8,91,4,4,64]{2,5,3,0,4,1:T(8,128)(2,1)} %bitcast.576) | data formatting | bytes 8945664 | tf_op jit(solution)/shard_map/transpose | solution.py:57
  460.2 10.7 %reshape.197 = bf16[3,728,1024]{1,2,0:T(8,128)(2,1)} reshape(bf16[3,8,91,4,4,64]{2,1,5,4,3,0:T(8,128)(2,1)} %copy.39) | data formatting | bytes 8945664 | tf_op jit(solution)/shard_map/reshape | solution.py:58
  470.8 8.1 %copy.45 = bf16[32,91,3,256]{1,3,2,0:T(8,128)(2,1)} copy(bf16[32,91,3,256]{3,1,2,0:T(8,128)(2,1)} %all-to-all-done.1) | data formatting | bytes 8945664 | tf_op jit(solution)/shard_map/all_to_all | solution.py:52
  478.9 18.1 %copy.46 = bf16[3,8,91,4,4,64]{2,1,5,4,3,0:T(8,128)(2,1)} copy(bf16[3,8,91,4,4,64]{2,5,3,0,4,1:T(8,128)(2,1)} %bitcast.577) | data formatting | bytes 8945664 | tf_op jit(solution)/shard_map/transpose | solution.py:57
  497.0 10.7 %reshape.199 = bf16[3,728,1024]{1,2,0:T(8,128)(2,1)} reshape(bf16[3,8,91,4,4,64]{2,1,5,4,3,0:T(8,128)(2,1)} %copy.46) | data formatting | bytes 8945664 | tf_op jit(solution)/shard_map/reshape | solution.py:58
  507.7 6.6 fusion.24
  514.3 6.6 fusion.27
  520.9 3.9 fusion.14
  524.8 6.3 reshape.179
  531.1 6.4 reshape.183
  537.5 8.4 %copy.52 = bf16[32,91,3,256]{1,3,2,0:T(8,128)(2,1)} copy(bf16[32,91,3,256]{3,1,2,0:T(8,128)(2,1)} %all-to-all-done.2) | data formatting | bytes 8945664 | tf_op jit(solution)/shard_map/all_to_all | solution.py:52
  545.9 18.1 %copy.53 = bf16[3,8,91,4,4,64]{2,1,5,4,3,0:T(8,128)(2,1)} copy(bf16[3,8,91,4,4,64]{2,5,3,0,4,1:T(8,128)(2,1)} %bitcast.578) | data formatting | bytes 8945664 | tf_op jit(solution)/shard_map/transpose | solution.py:57
  564.0 10.7 %reshape.201 = bf16[3,728,1024]{1,2,0:T(8,128)(2,1)} reshape(bf16[3,8,91,4,4,64]{2,1,5,4,3,0:T(8,128)(2,1)} %copy.53) | data formatting | bytes 8945664 | tf_op jit(solution)/shard_map/reshape | solution.py:58
  574.7 10.5 %fusion.30 = f32[3,721,1024]{2,1,0:T(8,128)} fusion(bf16[3,728,1024]{1,2,0:T(8,128)(2,1)} %reshape.201, bf16[12,721,728]{2,1,0:T(8,128)(2,1)} %param.8), kind=kOutput, calls=%fused_computation.35 | convolution fusion | flops 3224911872 | bytes 16932864 | tf_op jit(solution)/shard_map/brl,bln->brn/dot_general | solution.py:59
  585.2 8.1 %copy.59 = bf16[32,91,3,256]{1,3,2,0:T(8,128)(2,1)} copy(bf16[32,91,3,256]{3,1,2,0:T(8,128)(2,1)} %all-to-all-done.3) | data formatting | bytes 8945664 | tf_op jit(solution)/shard_map/all_to_all | solution.py:52
  593.3 18.2 %copy.60 = bf16[3,8,91,4,4,64]{2,1,5,4,3,0:T(8,128)(2,1)} copy(bf16[3,8,91,4,4,64]{2,5,3,0,4,1:T(8,128)(2,1)} %bitcast.579) | data formatting | bytes 8945664 | tf_op jit(solution)/shard_map/transpose | solution.py:57
  611.5 10.8 %reshape.203 = bf16[3,728,1024]{1,2,0:T(8,128)(2,1)} reshape(bf16[3,8,91,4,4,64]{2,1,5,4,3,0:T(8,128)(2,1)} %copy.60) | data formatting | bytes 8945664 | tf_op jit(solution)/shard_map/reshape | solution.py:58
  622.2 10.8 %fusion.33 = f32[3,721,1024]{2,1,0:T(8,128)} fusion(bf16[3,728,1024]{1,2,0:T(8,128)(2,1)} %reshape.203, bf16[12,721,728]{2,1,0:T(8,128)(2,1)} %param.8), kind=kOutput, calls=%fused_computation.36 | convolution fusion | flops 3224911872 | bytes 16932864 | tf_op jit(solution)/shard_map/brl,bln->brn/dot_general | solution.py:59
  633.0 8.3 %fusion.12 = (f32[3,721,512]{2,1,0:T(8,128)}, f32[3,721,512]{2,1,0:T(8,128)}) fusion(f32[3,721,1024]{2,1,0:T(8,128)} %fusion.33, f32[3]{0:T(128)S(1)} %get-tuple-element.17, pred[3,721]{1,0:T(4,128)(4,1)S(1)} %iota_compare_fusion, f32[3]{0:T(128)S(1)} %get-tuple-element.18, f32[3,721,1024]{2,1,0:T(8,128)S(1)} %bitcast.709, ...), kind=kLoop, calls=%fused_computation.18 | loop fusion | flops 4429824 | bytes 26583294 | tf_op jit(solution)/shard_map/mul | solution.py:70
  641.4 6.4 reshape.187
  647.8 6.4 reshape.191
  654.2 13.8 %pad_maximum_fusion = f32[12,721,2,256]{3,2,1,0:T(2,128)} fusion(f32[3,721,2,256]{3,2,1,0:T(2,128)} %reshape.191, f32[3,721,2,256]{3,2,1,0:T(2,128)} %reshape.187, f32[3,721,2,256]{3,2,1,0:T(2,128)} %reshape.183, f32[3,721,2,256]{3,2,1,0:T(2,128)} %reshape.179), kind=kLoop, calls=%fused_computation | loop fusion | flops 13289472 | bytes 35438592 | tf_op jit(solution)/shard_map/concatenate | solution.py:72
  (175 shorter events, 142.6 us)
Async XLA Ops:
  51.5 26.3 %copy-start = (bf16[91,384,64]{0,2,1:T(8,128)(2,1)S(1)}, bf16[91,384,64]{0,2,1:T(8,128)(2,1)}, u32[]{:S(2)}) copy-start(bf16[91,384,64]{0,2,1:T(8,128)(2,1)} %copy.36) | copy-start | bytes 13418500
  97.3 113.0 %all-to-all-start = ((bf16[32,91,3,256]{3,1,2,0:T(8,128)(2,1)}), bf16[32,91,3,256]{3,1,2,0:T(8,128)(2,1)}, u32[]{:S(2)}, u32[]{:S(2)}) async-start(bf16[32,91,3,256]{3,1,2,0:T(8,128)(2,1)} %copy.37), calls=%async_computation | async-start | bytes 9437184 | tf_op jit(solution)/shard_map/all_to_all | solution.py:52
  155.5 26.3 %copy-start.1 = (bf16[91,384,64]{0,2,1:T(8,128)(2,1)S(1)}, bf16[91,384,64]{0,2,1:T(8,128)(2,1)}, u32[]{:S(2)}) copy-start(bf16[91,384,64]{0,2,1:T(8,128)(2,1)} %copy.43) | copy-start | bytes 13418500
  210.2 109.3 %all-to-all-start.1 = ((bf16[32,91,3,256]{3,1,2,0:T(8,128)(2,1)}), bf16[32,91,3,256]{3,1,2,0:T(8,128)(2,1)}, u32[]{:S(2)}, u32[]{:S(2)}) async-start(bf16[32,91,3,256]{3,1,2,0:T(8,128)(2,1)} %copy.44), calls=%async_computation.1 | async-start | bytes 9437184 | tf_op jit(solution)/shard_map/all_to_all | solution.py:52
  264.3 26.3 %copy-start.2 = (bf16[91,384,64]{0,2,1:T(8,128)(2,1)S(1)}, bf16[91,384,64]{0,2,1:T(8,128)(2,1)}, u32[]{:S(2)}) copy-start(bf16[91,384,64]{0,2,1:T(8,128)(2,1)} %copy.50) | copy-start | bytes 13418500
  319.6 109.4 %all-to-all-start.2 = ((bf16[32,91,3,256]{3,1,2,0:T(8,128)(2,1)}), bf16[32,91,3,256]{3,1,2,0:T(8,128)(2,1)}, u32[]{:S(2)}, u32[]{:S(2)}) async-start(bf16[32,91,3,256]{3,1,2,0:T(8,128)(2,1)} %copy.51), calls=%async_computation.2 | async-start | bytes 9437184 | tf_op jit(solution)/shard_map/all_to_all | solution.py:52
  373.6 26.3 %copy-start.3 = (bf16[91,384,64]{0,2,1:T(8,128)(2,1)S(1)}, bf16[91,384,64]{0,2,1:T(8,128)(2,1)}, u32[]{:S(2)}) copy-start(bf16[91,384,64]{0,2,1:T(8,128)(2,1)} %copy.57) | copy-start | bytes 13418500
  419.3 13.8 %copy-start.4 = (s32[384]{0:T(512)S(1)}, s32[384]{0:T(512)}, u32[]{:S(2)}) copy-start(s32[384]{0:T(512)} %param.9) | copy-start | bytes 4612
  428.9 156.3 %all-to-all-start.3 = ((bf16[32,91,3,256]{3,1,2,0:T(8,128)(2,1)}), bf16[32,91,3,256]{3,1,2,0:T(8,128)(2,1)}, u32[]{:S(2)}, u32[]{:S(2)}) async-start(bf16[32,91,3,256]{3,1,2,0:T(8,128)(2,1)} %copy.58), calls=%async_computation.3 | async-start | bytes 9437184 | tf_op jit(solution)/shard_map/all_to_all | solution.py:52
  611.5 21.6 %slice-start = ((s8[8945664]{0:T(1024)(128)(4,1)}), s8[557056]{0:T(1024)(128)(4,1)S(1)}, s32[]{:S(2)}) async-start(s8[8945664]{0:T(1024)(128)(4,1)} %bitcast.708), calls=%async_computation.4 | async-start | bytes 1114112
  622.2 10.8 %slice-start.1 = ((s8[8945664]{0:T(1024)(128)(4,1)}), s8[4194304]{0:T(1024)(128)(4,1)S(1)}, s32[]{:S(2)}) async-start(s8[8945664]{0:T(1024)(128)(4,1)} %bitcast.708), calls=%async_computation.5 | async-start | bytes 8388608
  622.2 10.8 %slice-start.2 = ((s8[8945664]{0:T(1024)(128)(4,1)}), s8[4194304]{0:T(1024)(128)(4,1)S(1)}, s32[]{:S(2)}) async-start(s8[8945664]{0:T(1024)(128)(4,1)} %bitcast.708), calls=%async_computation.6 | async-start | bytes 8388608
